TPU v7x, 32 devices: a whole 2x2x4 slice. The times are simulated.
32 devices in a mesh: shard: 8 (over z, y), width: 4 (over x, core).
Axes of the slice: x: 2, y: 2, z: 4, core: 2. Of those that a mesh axis runs over, the one named last changes fastest.
Arguments:
- weight_gate: float32 [2048, 8192], P('shard', 'width'), may hold values from -0.1875 to 0.1875
- moment_gate: float32 [2048, 8192], P('shard', 'width'), may hold values from -6 to 6
- square_gate: float32 [2048, 8192], P('shard', 'width'), may hold values from 0.1 to 10
- weight_up: float32 [2048, 8192], P('shard', 'width'), may hold values from -0.1875 to 0.1875
- moment_up: float32 [2048, 8192], P('shard', 'width'), may hold values from -6 to 6
- square_up: float32 [2048, 8192], P('shard', 'width'), may hold values from 0.1 to 10
- norm_train: float32 [2048], P(('shard', 'width')), may hold values from 0.25 to 1.75
- norm_step: float32 [2048], P(('shard', 'width')), may hold values from -0.3 to 0.3
Outputs:
- serving_gate: bfloat16 [2048, 8192], P(None, 'width')
- serving_up: bfloat16 [2048, 8192], P(None, 'width')
- scale_gate: float32 [8192], P('width')
- scale_up: float32 [8192], P('width')
- serve_norm: bfloat16 [2048], replicated
- whole_gate: float32 [2048, 8192], P('shard', 'width')
- whole_up: float32 [2048, 8192], P('shard', 'width')
All inputs are finite; a program needn't handle non-finite values. Where the computation divides by a largest or mean magnitude, that divisor is 1e-20 or more.
Results may differ from a plain program's by a relative error of at most 0.001.
Values may be sent and summed in bfloat16 or wider, within the bound.
A program may use at most 128 MiB of HBM per device.

v0:
```python
import jax
import jax.numpy as jnp
from jax import lax
from jax.sharding import PartitionSpec as P

learn_rate = 0.02
decay_rate = 0.1
tiny_value = 1e-08


def body(
    weight_gate, moment_gate, square_gate, weight_up, moment_up, square_up, norm_train, norm_step
):
    whole_gate = weight_gate - learn_rate * (
        moment_gate / (jnp.sqrt(square_gate) + tiny_value) + decay_rate * weight_gate
    )
    whole_up = weight_up - learn_rate * (
        moment_up / (jnp.sqrt(square_up) + tiny_value) + decay_rate * weight_up
    )
    scale_gate, scale_up = lax.pmax(
        (jnp.max(jnp.abs(whole_gate), axis=0), jnp.max(jnp.abs(whole_up), axis=0)), "shard"
    )
    narrow_gate, narrow_up = (
        (whole_gate / scale_gate).astype(jnp.bfloat16),
        (whole_up / scale_up).astype(jnp.bfloat16),
    )
    serving_gate, serving_up = (
        lax.all_gather(narrow_gate, "shard", axis=0, tiled=True),
        lax.all_gather(narrow_up, "shard", axis=0, tiled=True),
    )
    serve_norm = lax.all_gather(
        (norm_train + norm_step).astype(jnp.bfloat16), ("shard", "width"), axis=0, tiled=True
    )
    return (serving_gate, serving_up, scale_gate, scale_up, serve_norm, whole_gate, whole_up)


def solution(mesh):
    return jax.shard_map(
        body,
        mesh=mesh,
        in_specs=(
            P("shard", "width"),
            P("shard", "width"),
            P("shard", "width"),
            P("shard", "width"),
            P("shard", "width"),
            P("shard", "width"),
            P(("shard", "width")),
            P(("shard", "width")),
        ),
        out_specs=(
            P(None, "width"),
            P(None, "width"),
            P("width"),
            P("width"),
            P(),
            P("shard", "width"),
            P("shard", "width"),
        ),
        check_vma=False,
    )
```

profile of v0, /device:TPU:0, one launch (start us, length us, event | category | flops | bytes accessed | tf_op | source)
XLA Modules:
  0.0 327.3 jit_solution(8631898927393345650)
XLA Ops:
  7.2 0.0 all-gather.5.cloned.1.call-start
  7.2 8.0 %abs_reduce_fusion = (f32[2048]{0:T(1024)S(1)}, f32[256,2048]{1,0:T(8,128)S(1)}, f32[2048]{0:T(1024)S(1)}, f32[256,2048]{1,0:T(8,128)}) fusion(f32[256,2048]{1,0:T(8,128)} %param.11, f32[256,2048]{1,0:T(8,128)} %param.12, f32[256,2048]{1,0:T(8,128)} %param.13, f32[256,2048]{1,0:T(8,128)} %param.8, f32[256,2048]{1,0:T(8,128)} %param.9, f32[256,2048]{1,0:T(8,128)} %param.10), kind=kLoop, calls=%fused_computation.1 | loop fusion | flops 8384512 | bytes 16793600 | tf_op jit(solution)/shard_map/reduce_max | solution.py:21
  15.2 0.0 copy-start
  15.2 38.9 %all-reduce.1 = (f32[2048]{0:T(1024)S(1)}, f32[2048]{0:T(1024)S(1)}) all-reduce(f32[2048]{0:T(1024)S(1)} %get-tuple-element.13, f32[2048]{0:T(1024)S(1)} %get-tuple-element.9), channel_id=1, replica_groups=mesh['shard'=8,'width'=4] {'shard'}, use_global_device_ids=true, to_apply=%region_1.0 | all-reduce | flops 4096 | bytes 32768 | tf_op jit(solution)/shard_map/pmax | solution.py:20
  54.1 0.0 copy-start.2
  54.1 0.0 copy-start.1
  54.1 1.2 divide_convert_fusion
  55.2 0.0 all-gather.5.cloned.1.call-update
  55.2 0.0 copy-done
  55.3 0.0 copy-done.2
  55.3 0.0 all-gather.3.cloned.1.call-start
  55.3 0.0 copy-done.1
  55.3 0.0 copy-start.3
  55.3 0.0 copy-start.4
  55.4 2.8 divide_convert_fusion.1
  58.1 0.0 all-gather.3.cloned.1.call-update
  58.1 0.0 copy-done.3
  58.1 0.0 copy-done.4
  58.2 0.2 dynamic-update-slice
  58.4 40.7 %all-reduce = bf16[2048]{0:T(1024)(128)(2,1)} all-reduce(bf16[2048]{0:T(1024)(128)(2,1)S(1)} %dynamic-update-slice), channel_id=1, replica_groups=mesh['shard'=8,'width'=4] {'shard','width'}, use_global_device_ids=true, to_apply=%add | all-reduce | flops 2048 | bytes 8192
  99.1 79.1 %all-gather.5.cloned.1.call-done = bf16[2048,2048]{1,0:T(8,128)(2,1)} async-done(((bf16[256,2048]{1,0:T(8,128)(2,1)}), bf16[2048,2048]{1,0:T(8,128)(2,1)}) %all-gather.5.cloned.1.call-update) | async-done | bytes 8388624 | tf_op jit(solution)/shard_map/all_gather | solution.py:29
  178.2 125.4 %all-gather.3.cloned.1.call-done = bf16[2048,2048]{1,0:T(8,128)(2,1)} async-done(((bf16[256,2048]{1,0:T(8,128)(2,1)}), bf16[2048,2048]{1,0:T(8,128)(2,1)}) %all-gather.3.cloned.1.call-update) | async-done | bytes 8388624 | tf_op jit(solution)/shard_map/all_gather | solution.py:28
  303.6 8.4 %copy.18 = bf16[2048,2048]{1,0:T(8,128)(2,1)} copy(bf16[2048,2048]{1,0:T(8,128)(2,1)} %all-gather.3.cloned.1.call-done) | data formatting | bytes 16777216
  312.0 8.4 %copy.19 = bf16[2048,2048]{1,0:T(8,128)(2,1)} copy(bf16[2048,2048]{1,0:T(8,128)(2,1)} %all-gather.5.cloned.1.call-done) | data formatting | bytes 16777216
  (2 shorter events, 0.0 us)
Async XLA Ops:
  7.2 171.0 %all-gather.5.cloned.1.call-start = ((), (), s32[]{:S(2)}) async-start(), calls=%async_computation.1 | async-start | bytes 9437184 | tf_op jit(solution)/shard_map/all_gather | solution.py:29
  15.2 40.1 %copy-start = (f32[256,2048]{1,0:T(8,128)}, f32[256,2048]{1,0:T(8,128)S(1)}, u32[]{:S(2)}) copy-start(f32[256,2048]{1,0:T(8,128)S(1)} %get-tuple-element.28) | copy-start | bytes 6291460
  54.1 1.2 copy-start.2
  54.1 1.3 copy-start.1
  55.3 248.3 %all-gather.3.cloned.1.call-start = ((), (), s32[]{:S(2)}) async-start(), calls=%async_computation | async-start | bytes 9437184 | tf_op jit(solution)/shard_map/all_gather | solution.py:28
  55.3 2.8 copy-start.3
  55.3 2.8 copy-start.4
Sparse Core Ops, SparseCore 0:
  55.4 122.7 all-gather.4
  180.9 122.6 all-gather.2
where the time goes:
time: 328 us; the launch traced here: 327 us
  waiting for transfers between devices  205 us (62%)
  blocking collectives  79.5 us (24%)
  local copies, waits for them, and re-layouts  17.2 us (5%)
  between operations  14.1 us (4%)
  other arithmetic  11.9 us (4%)
    all_gather x1, waiting for transfers between devices, body(): lax.all_gather(narrow_gate, 'shard', axis=0, tiled=True)  125 us
    all_gather x1, waiting for transfers between devices, body(): lax.all_gather(narrow_up, 'shard', axis=0, tiled=True)  79.1 us
    unnamed x1, blocking collectives  40.7 us
    pmax x1, blocking collectives, body(): lax.pmax((jnp.max(jnp.abs(whole_gate), axis=0), jnp.max(jnp.abs(whole_up)...  38.9 us
    unnamed x14, local copies, waits for them, and re-layouts  17.2 us
    reduce_max x1, other arithmetic, body(): jnp.max(jnp.abs(whole_up), axis=0)  7.98 us
  transfers between devices with their start and end apart: 2, of which 2 were waited for; matrix products, arithmetic and copies ran while one was open for 1% of the time, Pallas kernels for 0%

commit v1 on v0

v1 whole, which is shorter than its diff:
```python
import functools
import math

import jax
import jax.numpy as jnp
from jax import lax
from jax.experimental import pallas as pl
from jax.experimental.pallas import tpu as pltpu
from jax.sharding import PartitionSpec as P

MESH = pl.DeviceIdType.MESH
learn_rate = 0.02
decay_rate = 0.1
tiny_value = 1e-08


def gather_kernel(
    n, width, layers, group, rows, per, a_count, k_count,
    wg, wu, mx, piece, out, scale_ref, nb,
    wbuf, narrow, maxbuf, in_sem, own_sem, ms, mr, ns1, nr1, ns2, nr2, np_sem, zs, os, ys, rs,
):
    s, w = lax.axis_index("shard"), lax.axis_index("width")
    z, g = s // group, lax.rem(s, group)
    loads = [pltpu.make_async_copy(ref, wbuf.at[i], in_sem.at[i]) for i, ref in enumerate((wg, wu))]
    for load in loads:
        load.start()
    barrier = pltpu.get_barrier_semaphore()
    for j in range(1, n):
        pl.semaphore_signal(barrier, inc=1, device_id=(lax.rem(s + j, n), w), device_id_type=MESH)
    for j in range(1, width):
        pl.semaphore_signal(barrier, inc=1, device_id=(s, lax.rem(w + j, width)), device_id_type=MESH)
    pl.semaphore_wait(barrier, n - 1 + width - 1)

    def max_copy(j):
        return pltpu.make_async_remote_copy(
            mx, maxbuf.at[s], ms.at[j], mr.at[j], device_id=(lax.rem(s + j, n), w), device_id_type=MESH
        )

    def piece_copy(j):
        return pltpu.make_async_remote_copy(
            piece, nb.at[s, w], ns1.at[j], nr1.at[j], device_id=(s, lax.rem(w + j, width)), device_id_type=MESH
        )

    def norm_copy(j):
        return pltpu.make_async_remote_copy(
            nb.at[s], nb.at[s], ns2.at[j], nr2.at[j], device_id=(lax.rem(s + j, n), w), device_id_type=MESH
        )

    for j in range(1, n):
        max_copy(j).start()
    own_piece = pltpu.make_async_copy(piece, nb.at[s, w], np_sem.at[0])
    own_piece.start()
    for j in range(1, width):
        piece_copy(j).start()

    def place(source, k):
        return out.at[k // per, source, pl.ds(pl.multiple_of(lax.rem(k, per) * rows, rows), rows)]

    def own(k):
        return narrow.at[k // per, pl.ds(pl.multiple_of(lax.rem(k, per) * rows, rows), rows)]

    def copy(src, source, k, sem, device):
        return pltpu.make_async_remote_copy(
            src, place(source, k), sem, rs.at[source, k], device_id=(device, w), device_id_type=MESH
        )

    def partner(j):
        return z * group + lax.rem(g + j, group)

    def up(src, source, k, sem):
        return copy(src, source, k, sem.at[source, k], lax.rem(s + group, n))

    def down(src, source, k, sem):
        return copy(src, source, k, sem.at[source, k], lax.rem(s + n - group, n))

    def across(src, source, k, j):
        return copy(src, source, k, ys.at[j - 1, source, k], partner(j))

    def arrived(source, k):
        pltpu.make_async_copy(place(source, k), place(source, k), rs.at[source, k]).wait()

    for load in loads:
        load.wait()
    for j in range(1, n):
        max_copy(j).wait_recv()
    scale = mx[...]
    for j in range(1, n):
        scale = jnp.maximum(scale, maxbuf[lax.rem(s + n - j, n)])
    scale_ref[...] = scale

    def own_copy(k):
        return pltpu.make_async_copy(own(k), place(s, k), own_sem.at[k])

    def divide(k):
        a = k // per
        at = pl.ds(pl.multiple_of(lax.rem(k, per) * rows, rows), rows)
        narrow[a, at, :] = (wbuf[a, at, :] / scale_ref[pl.ds(a, 1), :]).astype(narrow.dtype)

    @pl.loop(0, k_count)
    def _(k):
        divide(k)

        @pl.when((k < a_count) & (z + 1 < layers))
        def _():
            up(own(k), s, k, zs).start()

        @pl.when((k < a_count) & (z > 0))
        def _():
            down(own(k), s, k, os).start()

        for j in range(1, group):
            across(own(k), s, k, j).start()
        own_copy(k).start()

    own_piece.wait()
    for j in range(1, width):
        piece_copy(j).wait_recv()
    for j in range(1, n):
        norm_copy(j).start()

    for d in range(1, layers):
        @pl.loop(0, a_count)
        def _(k):
            @pl.when(z - d >= 0)
            def _():
                source = s - d * group
                arrived(source, k)

                @pl.when(z + 1 < layers)
                def _():
                    up(place(source, k), source, k, zs).start()

                for j in range(1, group):
                    across(place(source, k), source, k, j).start()

            @pl.when(z + d < layers)
            def _():
                source = s + d * group
                arrived(source, k)

                @pl.when(z > 0)
                def _():
                    down(place(source, k), source, k, zs).start()

                for j in range(1, group):
                    across(place(source, k), source, k, j).start()

    for j in range(group):
        source = partner(j)

        @pl.loop(a_count, k_count)
        def _(k):
            if j:
                arrived(source, k)
            src = place(source, k) if j else own(k)

            @pl.when(z + 1 < layers)
            def _():
                up(src, source, k, zs).start()

            @pl.when(z > 0)
            def _():
                down(src, source, k, os).start()

    for d in range(1, layers):
        for j in range(group):
            @pl.loop(a_count, k_count)
            def _(k):
                @pl.when(z - d >= 0)
                def _():
                    source = partner(j) - d * group
                    arrived(source, k)

                    @pl.when(z + 1 < layers)
                    def _():
                        up(place(source, k), source, k, zs).start()

                @pl.when(z + d < layers)
                def _():
                    source = partner(j) + d * group
                    arrived(source, k)

                    @pl.when(z > 0)
                    def _():
                        down(place(source, k), source, k, zs).start()

    for j in range(1, group):
        @pl.loop(0, layers)
        def _(layer):
            @pl.loop(0, a_count)
            def _(k):
                arrived(layer * group + lax.rem(g + j, group), k)

    @pl.loop(0, k_count)
    def _(k):
        own_copy(k).wait()

        @pl.loop(0, layers)
        def _(layer):
            for j in range(group):
                source = layer * group + lax.rem(g + j, group)
                along = (k < a_count) if j == 0 else (k < 0)
                moved = along | (k >= a_count)

                @pl.when(moved & (layer <= z) & (z + 1 < layers))
                def _():
                    up(place(source, k), source, k, zs).wait_send()

                @pl.when(moved & (layer > z) & (z > 0))
                def _():
                    down(place(source, k), source, k, zs).wait_send()

                @pl.when(moved & (layer == z) & (z > 0))
                def _():
                    down(place(source, k), source, k, os).wait_send()

            @pl.when((k < a_count) | (layer == z))
            def _():
                for j in range(1, group):
                    source = layer * group + g
                    across(place(source, k), source, k, j).wait_send()

    for j in range(1, width):
        piece_copy(j).wait_send()
    for j in range(1, n):
        max_copy(j).wait_send()
        norm_copy(j).wait()


def solution(mesh):
    n, width = mesh.shape["shard"], mesh.shape["width"]
    layers = math.gcd(n, math.isqrt(2 * n))
    group = n // layers

    def body(
        weight_gate, moment_gate, square_gate, weight_up, moment_up, square_up, norm_train, norm_step
    ):
        whole_gate = weight_gate - learn_rate * (
            moment_gate / (jnp.sqrt(square_gate) + tiny_value) + decay_rate * weight_gate
        )
        whole_up = weight_up - learn_rate * (
            moment_up / (jnp.sqrt(square_up) + tiny_value) + decay_rate * weight_up
        )
        local = jnp.stack([jnp.max(jnp.abs(whole_gate), axis=0), jnp.max(jnp.abs(whole_up), axis=0)])
        count = norm_train.shape[0]
        lanes = -(-count // 128) * 128
        piece = jnp.pad((norm_train + norm_step)[None, :], ((0, 7), (0, lanes - count)))
        held, columns = whole_gate.shape
        per = max(1, min(held // 16, 64 // n))
        rows = held // per
        k_count = 2 * per
        a_count = k_count - max(1, round(k_count / 6))
        any_space = pl.BlockSpec(memory_space=pl.ANY)
        vmem_space = pl.BlockSpec(memory_space=pltpu.VMEM)
        dma = pltpu.SemaphoreType.DMA
        out, scale, nb = pl.pallas_call(
            functools.partial(gather_kernel, n, width, layers, group, rows, per, a_count, k_count),
            out_shape=(
                jax.ShapeDtypeStruct((2, n, held, columns), jnp.bfloat16),
                jax.ShapeDtypeStruct((2, columns), jnp.float32),
                jax.ShapeDtypeStruct((n, width, 8, lanes), jnp.float32),
            ),
            in_specs=[any_space, any_space, vmem_space, vmem_space],
            out_specs=(any_space, vmem_space, any_space),
            scratch_shapes=[
                pltpu.VMEM((2, held, columns), jnp.float32),
                pltpu.VMEM((2, held, columns), jnp.bfloat16),
                pltpu.VMEM((n, 2, columns), jnp.float32),
                dma((2,)),
                dma((k_count,)),
                dma((n,)),
                dma((n,)),
                dma((width,)),
                dma((width,)),
                dma((n,)),
                dma((n,)),
                dma((1,)),
                dma((n, k_count)),
                dma((n, k_count)),
                dma((max(1, group - 1), n, k_count)),
                dma((n, k_count)),
            ],
            compiler_params=pltpu.CompilerParams(collective_id=0, has_side_effects=True),
            name="gather",
        )(whole_gate, whole_up, local, piece)
        serve_norm = nb[:, :, 0, :count].reshape(-1).astype(jnp.bfloat16)
        return (
            out[0].reshape(n * held, columns),
            out[1].reshape(n * held, columns),
            scale[0],
            scale[1],
            serve_norm,
            whole_gate,
            whole_up,
        )

    return jax.shard_map(
        body,
        mesh=mesh,
        in_specs=(P("shard", "width"),) * 6 + (P(("shard", "width")),) * 2,
        out_specs=(
            P(None, "width"),
            P(None, "width"),
            P("width"),
            P("width"),
            P(),
            P("shard", "width"),
            P("shard", "width"),
        ),
        check_vma=False,
    )
```

time: 328 us -> 208 us (0.63)
  waiting for transfers between devices: 205 us -> 0 us
  Pallas kernels: 0 us -> 182 us
  blocking collectives: 79.5 us -> 0 us
  between operations: 14.1 us -> 0.65 us
    all_gather x2 -> x0, waiting for transfers between devices: 204 us -> none  [the longest x1 125 us: body(): lax.all_gather(narrow_gate, 'shard', axis=0, tiled=True)]
    pallas_call x0 -> x1, Pallas kernels: none -> 182 us  [body(): pl.pallas_call(functools.partial(gather_kernel, n, width, layers, group,...]
    unnamed x1 -> x0, blocking collectives: 40.7 us -> none
    pmax x1 -> x0, blocking collectives: 38.9 us -> none  [body(): lax.pmax((jnp.max(jnp.abs(whole_gate), axis=0), jnp.max(jnp.abs(whole_up)...]
    unnamed x14 -> x2, local copies, waits for them, and re-layouts: 17.2 us -> 0.01 us
    slice x0 -> x3, local copies, waits for them, and re-layouts: none -> 13.5 us  [the longest x1 12 us: body(): out[1].reshape(n * held, columns)]
    convert_element_type x3 -> x0, other arithmetic: 3.92 us -> none  [the longest x1 2.76 us: body(): (whole_gate / scale_gate).astype(jnp.bfloat16)]
  transfers between devices with their start and end apart: 2 -> 0, of which waited for: 2 -> 0; matrix products, arithmetic and copies ran while one was open for 1% -> 0% of each run, Pallas kernels for 0% -> 0%
where the time goes in v1:
time: 208 us; the launch traced here: 207 us
  Pallas kernels  182 us (88%)
  local copies, waits for them, and re-layouts  14.8 us (7%)
  other arithmetic  9.97 us (5%)
    pallas_call x1, Pallas kernels, body(): pl.pallas_call(functools.partial(gather_kernel, n, width, layers, group,...  182 us
    slice x1, local copies, waits for them, and re-layouts, body(): out[1].reshape(n * held, columns)  12 us
    reduce_max x1, other arithmetic, body(): jnp.max(jnp.abs(whole_up), axis=0)  8.67 us

profile of v1, /device:TPU:0, one launch (start us, length us, event | category | flops | bytes accessed | tf_op | source)
XLA Modules:
  0.0 207.4 jit_solution(5036864609599296896)
XLA Ops:
  0.6 0.7 add_bitcast_fusion
  1.3 0.6 pad.4.piece
  1.9 8.7 %abs_reduce_fusion = (f32[2048]{0:T(1024)S(1)}, f32[256,2048]{1,0:T(8,128)}, f32[2048]{0:T(1024)S(1)}, f32[256,2048]{1,0:T(8,128)}) fusion(f32[256,2048]{1,0:T(8,128)} %param.11, f32[256,2048]{1,0:T(8,128)} %param.12, f32[256,2048]{1,0:T(8,128)} %param.13, f32[256,2048]{1,0:T(8,128)} %param.8, f32[256,2048]{1,0:T(8,128)} %param.9, f32[256,2048]{1,0:T(8,128)} %param.10), kind=kLoop, calls=%fused_computation | loop fusion | flops 8384512 | bytes 16793600 | tf_op jit(solution)/shard_map/reduce_max | solution.py:244
  10.6 0.6 pad_maximum_fusion.mx
  11.2 182.0 %gather.1 = (bf16[2,8,256,2048]{3,2,1,0:T(8,128)(2,1)}, f32[2,2048]{1,0:T(2,128)}, f32[8,4,8,128]{3,2,1,0:T(8,128)}) custom-call(f32[256,2048]{1,0:T(8,128)} %get-tuple-element.22.wg, f32[256,2048]{1,0:T(8,128)} %get-tuple-element.16.wu, f32[2,2048]{1,0:T(2,128)} %pad_maximum_fusion.mx, f32[8,128]{1,0:T(8,128)} %pad.4.piece), custom_call_target="tpu_custom_call" | custom-call | tf_op jit(solution)/shard_map/gather/pallas_call | solution.py:256
  193.2 0.0 copy-start
  193.2 12.0 %fusion.1 = (bf16[1,8,256,2048]{3,2,1,0:T(8,128)(2,1)}, bf16[1,8,256,2048]{3,2,1,0:T(8,128)(2,1)}) fusion(bf16[2,8,256,2048]{3,2,1,0:T(8,128)(2,1)} %get-tuple-element.10), kind=kLoop, calls=%fused_computation.8 | loop fusion | bytes 33554432 | tf_op jit(solution)/shard_map/slice | solution.py:289
  205.2 1.0 fusion
  206.1 0.7 convert_element_type.6
  206.8 0.0 copy-done
  206.8 0.6 fusion.2
Async XLA Ops:
  193.2 13.6 %copy-start = (f32[2,2048]{1,0:T(2,128)S(1)}, f32[2,2048]{1,0:T(2,128)}, u32[]{:S(2)}) copy-start(f32[2,2048]{1,0:T(2,128)} %get-tuple-element.11) | copy-start | bytes 49156

commit v2 on v1

--- a/solution.py
+++ b/solution.py
@@ -12,16 +12,21 @@
 learn_rate = 0.02
 decay_rate = 0.1
 tiny_value = 1e-08
+UNIT = 16
+MOST = 9
 
 
 def gather_kernel(
-    n, width, layers, group, rows, per, a_count, k_count,
+    n, width, layers, group, rows, late_rows, a_count, k_count,
     wg, wu, mx, piece, out, scale_ref, nb,
     wbuf, narrow, maxbuf, in_sem, own_sem, ms, mr, ns1, nr1, ns2, nr2, np_sem, zs, os, ys, rs,
 ):
     s, w = lax.axis_index("shard"), lax.axis_index("width")
     z, g = s // group, lax.rem(s, group)
-    loads = [pltpu.make_async_copy(ref, wbuf.at[i], in_sem.at[i]) for i, ref in enumerate((wg, wu))]
+    held = wg.shape[0]
+    loads = [
+        pltpu.make_async_copy(ref, wbuf.at[pl.ds(i * held, held)], in_sem.at[i]) for i, ref in enumerate((wg, wu))
+    ]
     for load in loads:
         load.start()
     barrier = pltpu.get_barrier_semaphore()
@@ -53,31 +58,39 @@
     for j in range(1, width):
         piece_copy(j).start()
 
+    def span(k):
+        if isinstance(k, tuple):
+            return pl.ds(pl.multiple_of(a_count * rows + k[0] * late_rows, UNIT), late_rows)
+        return pl.ds(pl.multiple_of(k * rows, UNIT), rows)
+
+    def slot(k):
+        return a_count + k[0] if isinstance(k, tuple) else k
+
     def place(source, k):
-        return out.at[k // per, source, pl.ds(pl.multiple_of(lax.rem(k, per) * rows, rows), rows)]
+        return out.at[source, span(k)]
 
     def own(k):
-        return narrow.at[k // per, pl.ds(pl.multiple_of(lax.rem(k, per) * rows, rows), rows)]
+        return narrow.at[span(k)]
 
     def copy(src, source, k, sem, device):
         return pltpu.make_async_remote_copy(
-            src, place(source, k), sem, rs.at[source, k], device_id=(device, w), device_id_type=MESH
+            src, place(source, k), sem, rs.at[source, slot(k)], device_id=(device, w), device_id_type=MESH
         )
 
     def partner(j):
         return z * group + lax.rem(g + j, group)
 
     def up(src, source, k, sem):
-        return copy(src, source, k, sem.at[source, k], lax.rem(s + group, n))
+        return copy(src, source, k, sem.at[source, slot(k)], lax.rem(s + group, n))
 
     def down(src, source, k, sem):
-        return copy(src, source, k, sem.at[source, k], lax.rem(s + n - group, n))
+        return copy(src, source, k, sem.at[source, slot(k)], lax.rem(s + n - group, n))
 
     def across(src, source, k, j):
-        return copy(src, source, k, ys.at[j - 1, source, k], partner(j))
+        return copy(src, source, k, ys.at[j - 1, source, slot(k)], partner(j))
 
     def arrived(source, k):
-        pltpu.make_async_copy(place(source, k), place(source, k), rs.at[source, k]).wait()
+        pltpu.make_async_copy(place(source, k), place(source, k), rs.at[source, slot(k)]).wait()
 
     for load in loads:
         load.wait()
@@ -89,25 +102,38 @@
     scale_ref[...] = scale
 
     def own_copy(k):
-        return pltpu.make_async_copy(own(k), place(s, k), own_sem.at[k])
-
-    def divide(k):
-        a = k // per
-        at = pl.ds(pl.multiple_of(lax.rem(k, per) * rows, rows), rows)
-        narrow[a, at, :] = (wbuf[a, at, :] / scale_ref[pl.ds(a, 1), :]).astype(narrow.dtype)
-
-    @pl.loop(0, k_count)
+        return pltpu.make_async_copy(own(k), place(s, k), own_sem.at[slot(k)])
+
+    def divide(unit):
+        at = pl.ds(pl.multiple_of(unit * UNIT, UNIT), UNIT)
+        scaled = wbuf[at, :] / scale_ref[pl.ds(unit * UNIT // held, 1), :]
+        narrow[at, :] = scaled.astype(narrow.dtype)
+
+    @pl.loop(0, a_count)
     def _(k):
-        divide(k)
-
-        @pl.when((k < a_count) & (z + 1 < layers))
+        @pl.loop(0, rows // UNIT)
+        def _(u):
+            divide(k * (rows // UNIT) + u)
+
+        @pl.when(z + 1 < layers)
         def _():
             up(own(k), s, k, zs).start()
 
-        @pl.when((k < a_count) & (z > 0))
+        @pl.when(z > 0)
         def _():
             down(own(k), s, k, os).start()
 
+        for j in range(1, group):
+            across(own(k), s, k, j).start()
+        own_copy(k).start()
+
+    @pl.loop(a_count * rows // UNIT, 2 * held // UNIT)
+    def _(u):
+        divide(u)
+
+    @pl.loop(0, k_count - a_count)
+    def _(q):
+        k = (q,)
         for j in range(1, group):
             across(own(k), s, k, j).start()
         own_copy(k).start()
@@ -148,8 +174,9 @@
     for j in range(group):
         source = partner(j)
 
-        @pl.loop(a_count, k_count)
-        def _(k):
+        @pl.loop(0, k_count - a_count)
+        def _(q):
+            k = (q,)
             if j:
                 arrived(source, k)
             src = place(source, k) if j else own(k)
@@ -164,8 +191,10 @@
 
     for d in range(1, layers):
         for j in range(group):
-            @pl.loop(a_count, k_count)
-            def _(k):
+            @pl.loop(0, k_count - a_count)
+            def _(q):
+                k = (q,)
+
                 @pl.when(z - d >= 0)
                 def _():
                     source = partner(j) - d * group
@@ -191,34 +220,41 @@
             def _(k):
                 arrived(layer * group + lax.rem(g + j, group), k)
 
-    @pl.loop(0, k_count)
+    def left(source, k, layer):
+        @pl.when((layer <= z) & (z + 1 < layers))
+        def _():
+            up(place(source, k), source, k, zs).wait_send()
+
+        @pl.when((layer > z) & (z > 0))
+        def _():
+            down(place(source, k), source, k, zs).wait_send()
+
+        @pl.when((layer == z) & (z > 0))
+        def _():
+            down(place(source, k), source, k, os).wait_send()
+
+    @pl.loop(0, a_count)
     def _(k):
         own_copy(k).wait()
+
+        @pl.loop(0, layers)
+        def _(layer):
+            source = layer * group + g
+            left(source, k, layer)
+            for j in range(1, group):
+                across(place(source, k), source, k, j).wait_send()
+
+    @pl.loop(0, k_count - a_count)
+    def _(q):
+        k = (q,)
+        own_copy(k).wait()
+        for j in range(1, group):
+            across(own(k), s, k, j).wait_send()
 
         @pl.loop(0, layers)
         def _(layer):
             for j in range(group):
-                source = layer * group + lax.rem(g + j, group)
-                along = (k < a_count) if j == 0 else (k < 0)
-                moved = along | (k >= a_count)
-
-                @pl.when(moved & (layer <= z) & (z + 1 < layers))
-                def _():
-                    up(place(source, k), source, k, zs).wait_send()
-
-                @pl.when(moved & (layer > z) & (z > 0))
-                def _():
-                    down(place(source, k), source, k, zs).wait_send()
-
-                @pl.when(moved & (layer == z) & (z > 0))
-                def _():
-                    down(place(source, k), source, k, os).wait_send()
-
-            @pl.when((k < a_count) | (layer == z))
-            def _():
-                for j in range(1, group):
-                    source = layer * group + g
-                    across(place(source, k), source, k, j).wait_send()
+                left(layer * group + lax.rem(g + j, group), k, layer)
 
     for j in range(1, width):
         piece_copy(j).wait_send()
@@ -246,25 +282,27 @@
         lanes = -(-count // 128) * 128
         piece = jnp.pad((norm_train + norm_step)[None, :], ((0, 7), (0, lanes - count)))
         held, columns = whole_gate.shape
-        per = max(1, min(held // 16, 64 // n))
-        rows = held // per
-        k_count = 2 * per
-        a_count = k_count - max(1, round(k_count / 6))
+        units = 2 * held // UNIT
+        late_units = max(1, units * 5 // 32)
+        early_units = units - late_units
+        step = max(d for d in range(1, MOST + 1) if early_units % d == 0)
+        rows, late_rows = step * UNIT, late_units * UNIT
+        a_count, k_count = early_units // step, early_units // step + 1
         any_space = pl.BlockSpec(memory_space=pl.ANY)
         vmem_space = pl.BlockSpec(memory_space=pltpu.VMEM)
         dma = pltpu.SemaphoreType.DMA
         out, scale, nb = pl.pallas_call(
-            functools.partial(gather_kernel, n, width, layers, group, rows, per, a_count, k_count),
+            functools.partial(gather_kernel, n, width, layers, group, rows, late_rows, a_count, k_count),
             out_shape=(
-                jax.ShapeDtypeStruct((2, n, held, columns), jnp.bfloat16),
+                jax.ShapeDtypeStruct((n, 2 * held, columns), jnp.bfloat16),
                 jax.ShapeDtypeStruct((2, columns), jnp.float32),
                 jax.ShapeDtypeStruct((n, width, 8, lanes), jnp.float32),
             ),
             in_specs=[any_space, any_space, vmem_space, vmem_space],
             out_specs=(any_space, vmem_space, any_space),
             scratch_shapes=[
-                pltpu.VMEM((2, held, columns), jnp.float32),
-                pltpu.VMEM((2, held, columns), jnp.bfloat16),
+                pltpu.VMEM((2 * held, columns), jnp.float32),
+                pltpu.VMEM((2 * held, columns), jnp.bfloat16),
                 pltpu.VMEM((n, 2, columns), jnp.float32),
                 dma((2,)),
                 dma((k_count,)),
@@ -280,13 +318,15 @@
                 dma((max(1, group - 1), n, k_count)),
                 dma((n, k_count)),
             ],
-            compiler_params=pltpu.CompilerParams(collective_id=0, has_side_effects=True),
+            compiler_params=pltpu.CompilerParams(
+                collective_id=0, has_side_effects=True, vmem_limit_bytes=14 << 20
+            ),
             name="gather",
         )(whole_gate, whole_up, local, piece)
         serve_norm = nb[:, :, 0, :count].reshape(-1).astype(jnp.bfloat16)
         return (
-            out[0].reshape(n * held, columns),
-            out[1].reshape(n * held, columns),
+            out[:, :held].reshape(n * held, columns),
+            out[:, held:].reshape(n * held, columns),
             scale[0],
             scale[1],
             serve_norm,

time: 208 us -> 189 us (0.909)
  Pallas kernels: 182 us -> 173 us
  local copies, waits for them, and re-layouts: 14.8 us -> 7.75 us
  other arithmetic: 9.97 us -> 7.37 us
    pallas_call x1, Pallas kernels: 182 us -> 173 us  [body(): pl.pallas_call(functools.partial(gather_kernel, n, width, layers, group,...]
    slice x1, local copies, waits for them, and re-layouts: 12 us -> 6.39 us  [body(): out[:, held:].reshape(n * held, columns)]
where the time goes in v2:
time: 189 us
  Pallas kernels  173 us (92%)
  local copies, waits for them, and re-layouts  7.75 us (4%)
  other arithmetic  7.37 us (4%)
    pallas_call x1, Pallas kernels, body(): pl.pallas_call(functools.partial(gather_kernel, n, width, layers, group,...  173 us
    reduce_max x1, other arithmetic, body(): jnp.max(jnp.abs(whole_up), axis=0)  6.67 us
    slice x1, local copies, waits for them, and re-layouts, body(): out[:, held:].reshape(n * held, columns)  6.39 us

profile of v2, /device:TPU:0, one launch (start us, length us, event | category | flops | bytes accessed | tf_op | source)
XLA Modules:
  0.0 188.8 jit_solution(4487426726366271255)
XLA Ops:
  0.6 0.7 add_bitcast_fusion
  1.3 6.7 %abs_reduce_fusion = (f32[2048]{0:T(1024)S(1)}, f32[256,2048]{1,0:T(8,128)S(1)}, f32[2048]{0:T(1024)S(1)}, f32[256,2048]{1,0:T(8,128)S(1)}) fusion(f32[256,2048]{1,0:T(8,128)} %param.11, f32[256,2048]{1,0:T(8,128)} %param.12, f32[256,2048]{1,0:T(8,128)} %param.13, f32[256,2048]{1,0:T(8,128)} %param.8, f32[256,2048]{1,0:T(8,128)} %param.9, f32[256,2048]{1,0:T(8,128)} %param.10), kind=kLoop, calls=%fused_computation | loop fusion | flops 8384512 | bytes 16793600 | tf_op jit(solution)/shard_map/reduce_max | solution.py:280
  8.0 0.0 copy-start
  8.0 0.0 copy-start.1
  8.0 173.0 %gather.1 = (bf16[8,512,2048]{2,1,0:T(8,128)(2,1)S(1)}, f32[2,2048]{1,0:T(2,128)S(1)}, f32[8,4,8,128]{3,2,1,0:T(8,128)S(1)}) custom-call(f32[256,2048]{1,0:T(8,128)S(1)} %get-tuple-element.22.wg, f32[256,2048]{1,0:T(8,128)S(1)} %get-tuple-element.16.wu, f32[2,2048]{1,0:T(2,128)S(1)} %pad_maximum_fusion.mx, f32[8,128]{1,0:T(8,128)S(1)} %pad.4.piece), custom_call_target="tpu_custom_call" | custom-call | tf_op jit(solution)/shard_map/gather/pallas_call | solution.py:294
  181.0 0.0 copy-done
  181.0 0.0 copy-done.1
  181.1 6.4 %fusion.1 = (bf16[8,256,2048]{2,1,0:T(8,128)(2,1)}, bf16[8,256,2048]{2,1,0:T(8,128)(2,1)}) fusion(bf16[8,512,2048]{2,1,0:T(8,128)(2,1)S(1)} %get-tuple-element.10), kind=kLoop, calls=%fused_computation.8 | loop fusion | bytes 33554432 | tf_op jit(solution)/shard_map/slice | solution.py:329
  187.4 0.1 fusion
  187.5 0.7 convert_element_type.6
  188.2 0.6 fusion.2
  (2 shorter events, 0.0 us)
Async XLA Ops:
  8.0 173.0 %copy-start = (f32[256,2048]{1,0:T(8,128)}, f32[256,2048]{1,0:T(8,128)S(1)}, u32[]{:S(2)}) copy-start(f32[256,2048]{1,0:T(8,128)S(1)} %get-tuple-element.16.wu) | copy-start | bytes 6291460
  8.0 173.0 %copy-start.1 = (f32[256,2048]{1,0:T(8,128)}, f32[256,2048]{1,0:T(8,128)S(1)}, u32[]{:S(2)}) copy-start(f32[256,2048]{1,0:T(8,128)S(1)} %get-tuple-element.22.wg) | copy-start | bytes 6291460
